TPU v7x, 128 devices: a whole 4x4x4 slice. The times are simulated.
128 devices in a mesh: dp: 32 (over z, y, x_hi), expert: 2 (over core), tensor: 2 (over x_lo).
Axes of the slice: x: 4 (x_hi: 2, x_lo: 2; x = x_hi * 2 + x_lo), y: 4, z: 4, core: 2. Of those that a mesh axis runs over, the one named last changes fastest.
Arguments:
- dense_act: bfloat16 [2, 128, 512, 3584], P(None, 'dp', 'expert', 'tensor'), may hold values from -6 to 6
- dense_cot: bfloat16 [2, 128, 512, 3584], P(None, 'dp', ('expert', 'tensor')), may hold values from -6 to 6
- dense_proj_in: bfloat16 [2, 3584, 128], P(None, 'tensor'), may hold values from -0.09375 to 0.09375
- dense_proj_out: bfloat16 [2, 3584, 128], replicated, may hold values from -0.09375 to 0.09375
- expert_act: bfloat16 [128, 8, 64, 2560], P('dp', 'expert', None, 'tensor'), may hold values from -6 to 6
- expert_cot: bfloat16 [128, 8, 64, 3584], P('dp', 'expert', 'tensor'), may hold values from -6 to 6
- expert_proj_in: bfloat16 [2560, 128], P('tensor'), may hold values from -0.125 to 0.125
- expert_proj_out: bfloat16 [3584, 128], replicated, may hold values from -0.09375 to 0.09375
- dense_valid: float32 [2, 128, 128], replicated, may hold values from -0.0012207031 to 0.0012207031
- expert_valid: float32 [8, 128, 128], P('expert'), may hold values from -0.0012207031 to 0.0012207031
- domain_ids: int32 [128], P('dp'), may hold values from 0 to 63
- prior_mix: float32 [64], replicated, may hold values from 0.002 to 0.05
Outputs:
- log_mixture_weights: float32 [64], P('dp')
All inputs are finite; a program needn't handle non-finite values.
Results may differ from a plain program's by a relative error of at most 0.0003.
Values sent between devices are 32-bit elements; how exact they have to be, the bound alone decides.
A program may use at most 128 MiB of HBM per device.

v0:
```python
import jax
import jax.numpy as jnp
from jax import lax
from jax.sharding import PartitionSpec as P


def cut_along(array, dim, peers):
    before, after = (array.shape[:dim], array.shape[dim + 1 :])
    return jnp.moveaxis(array.reshape(*before, peers, -1, *after), dim, 0)


def sum_at_owner(array, axis, dim):
    tiles = cut_along(array, dim, lax.axis_size(axis))
    arrived = lax.all_to_all(tiles, axis, split_axis=0, concat_axis=0, tiled=True)
    return arrived.sum(axis=0)


def from_everyone(array, axis):
    peers = lax.axis_size(axis)
    return lax.all_to_all(
        jnp.broadcast_to(array[None], (peers, *array.shape)), axis, 0, 0, tiled=True
    )


def taken_together(array, axis):
    everything = from_everyone(array, axis)
    return jnp.sum(everything, axis=0)


def per_device(
    dense_act,
    dense_cot,
    dense_proj_in,
    dense_proj_out,
    expert_act,
    expert_cot,
    expert_proj_in,
    expert_proj_out,
    dense_valid,
    expert_valid,
    domain_ids,
    prior_mix,
):
    block = dense_act
    dense_update_vector = sum_at_owner(
        jnp.einsum("lmtd,ldr->tlmr", block, dense_proj_in, preferred_element_type=jnp.float32),
        "tensor",
        0,
    )
    dense_weight_matrix = jnp.einsum(
        "lmtd,ldr->tlmr", dense_cot, dense_proj_out, preferred_element_type=jnp.float32
    )
    dense_portion = jnp.einsum(
        "fquy,fquh->quyh", dense_update_vector, dense_weight_matrix, precision=lax.Precision.HIGHEST
    )
    block = expert_act
    expert_u = sum_at_owner(
        jnp.einsum("mecf,fr->cmer", block, expert_proj_in, preferred_element_type=jnp.float32),
        "tensor",
        0,
    )
    expert_weight_matrix = jnp.einsum(
        "mecd,dr->cmer", expert_cot, expert_proj_out, preferred_element_type=jnp.float32
    )
    expert_part = jnp.einsum(
        "cmer,cmes->mers", expert_u, expert_weight_matrix, precision=lax.Precision.HIGHEST
    )
    local_score = jnp.sum(dense_portion * dense_valid[:, None], axis=(0, 2, 3)) + jnp.sum(
        expert_part * expert_valid[None], axis=(1, 2, 3)
    )
    score = taken_together(local_score, ("expert", "tensor"))
    domains = prior_mix.shape[0]
    onehot = (domain_ids[:, None] == jnp.arange(domains, dtype=jnp.int32)[None, :]).astype(
        jnp.float32
    )
    domain_part = jnp.dot(score, onehot, precision=lax.Precision.HIGHEST)
    share_tally_count = domains // lax.axis_size("dp")
    first_domain = lax.axis_index("dp") * share_tally_count
    previous_domain_share = lax.dynamic_slice_in_dim(prior_mix, first_domain, share_tally_count, 0)
    domain_total = taken_together(domain_part, "dp")
    spread = jnp.sqrt(jnp.mean(domain_total * domain_total) + 1e-06)
    z_value = domain_total / spread
    mass = jnp.sum(prior_mix * jnp.exp(0.5 * z_value))
    z_share = lax.dynamic_slice_in_dim(z_value, first_domain, share_tally_count, 0)
    return jnp.log(previous_domain_share) + 0.5 * z_share - jnp.log(mass)


def solution(mesh):
    placed = (
        P(None, "dp", "expert", "tensor"),
        P(None, "dp", ("expert", "tensor"), None),
        P(None, "tensor", None),
        P(),
        P("dp", "expert", None, "tensor"),
        P("dp", "expert", "tensor", None),
        P("tensor", None),
        P(),
        P(),
        P("expert", None, None),
        P("dp"),
        P(),
    )
    return jax.shard_map(per_device, mesh=mesh, in_specs=placed, out_specs=P("dp"), check_vma=False)
```

profile of v0, /device:TPU:1, one launch (start us, length us, event | category | flops | bytes accessed | tf_op | source)
XLA Modules:
  0.0 71.7 jit_solution(239246663486171055)
XLA Ops:
  0.0 0.0 copy-start
  0.0 1.7 %copy-done = bf16[4,4,64,1280]{3,2,1,0:T(8,128)(2,1)S(1)} copy-done((bf16[4,4,64,1280]{3,2,1,0:T(8,128)(2,1)S(1)}, bf16[4,4,64,1280]{3,2,1,0:T(8,128)(2,1)}, u32[]{:S(2)}) %copy-start) | copy-done | bytes 2621464
  1.7 1.8 %fusion.10 = f32[128,4,4,64]{0,3,2,1:T(8,128)S(1)} fusion(bf16[4,4,64,1280]{3,2,1,0:T(8,128)(2,1)S(1)} %copy-done, bf16[1280,128]{1,0:T(8,128)(2,1)} %param.18), kind=kOutput, calls=%fused_computation.13 | convolution fusion | flops 335544320 | bytes 3473408 | tf_op jit(solution)/shard_map/mecf,fr->cmer/dot_general | solution.py:58
  3.6 0.8 %copy.31 = f32[2,32,4,4,128]{4,1,3,2,0:T(8,128)} copy(f32[2,32,4,4,128]{4,1,0,3,2:T(8,128)S(1)} %bitcast.49) | data formatting | bytes 1048576 | tf_op jit(solution)/shard_map/reshape | solution.py:9
  4.4 4.2 %all-to-all-start.1 = ((f32[2,32,4,4,128]{4,1,3,2,0:T(8,128)}), f32[2,32,4,4,128]{4,1,3,2,0:T(8,128)}, u32[]{:S(2)}, u32[]{:S(2)}) async-start(f32[2,32,4,4,128]{4,1,3,2,0:T(8,128)} %copy.31), calls=%async_computation.1 | async-start | bytes 1048576 | tf_op jit(solution)/shard_map/all_to_all | solution.py:14
  8.6 0.0 copy-start.1
  8.6 0.0 copy-start.2
  8.7 6.3 %fusion.3 = f32[128,2,4,128]{0,3,2,1:T(8,128)S(1)} fusion(bf16[2,4,128,3584]{3,2,1,0:T(8,128)(2,1)} %param.13, bf16[2,3584,128]{2,1,0:T(8,128)(2,1)} %param.15), kind=kOutput, calls=%fused_computation.5 | convolution fusion | flops 939524096 | bytes 9699328 | tf_op jit(solution)/shard_map/lmtd,ldr->tlmr/dot_general | solution.py:50
  15.0 0.0 copy-done.1
  15.0 0.0 copy-done.2
  15.0 2.5 %convolution_bitcast_fusion = f32[2,4,16,2,8,128]{5,4,3,2,1,0:T(8,128)S(1)} fusion(bf16[2,4,256,1792]{3,2,1,0:T(8,128)(2,1)S(1)} %copy-done.1, bf16[2,1792,128]{2,1,0:T(8,128)(2,1)S(1)} %copy-done.2), kind=kOutput, calls=%fused_computation.2 | convolution fusion | flops 939524096 | bytes 9306112 | tf_op jit(solution)/shard_map/lmtd,ldr->tlmr/dot_general | solution.py:46
  17.6 1.1 %copy.48 = f32[2,4,16,2,8,128]{5,4,2,1,0,3:T(8,128)} copy(f32[2,4,16,2,8,128]{5,4,3,2,1,0:T(8,128)S(1)} %convolution_bitcast_fusion) | data formatting | bytes 2097152 | tf_op jit(solution)/shard_map/reshape | solution.py:9
  18.7 0.0 all-to-all-done.1
  18.7 4.4 %all-to-all-start = ((f32[2,128,2,4,128]{1,4,3,2,0:T(8,128)}), f32[2,128,2,4,128]{1,4,3,2,0:T(8,128)}, u32[]{:S(2)}, u32[]{:S(2)}) async-start(f32[2,128,2,4,128]{1,4,3,2,0:T(8,128)} %bitcast.48), calls=%async_computation | async-start | bytes 2097152 | tf_op jit(solution)/shard_map/all_to_all | solution.py:14
  23.1 0.0 copy-start.3
  23.1 4.2 %fusion.8 = f32[128,4,4,32]{0,3,2,1:T(8,128)} fusion(bf16[4,4,32,3584]{3,2,1,0:T(8,128)(2,1)} %param.17, bf16[3584,128]{1,0:T(8,128)(2,1)} %param.19), kind=kOutput, calls=%fused_computation.11 | convolution fusion | flops 469762048 | bytes 4849664 | tf_op jit(solution)/shard_map/mecd,dr->cmer/dot_general | solution.py:62
  27.3 0.0 copy-start.5
  27.3 0.0 copy-start.4
  27.3 1.1 %reduce_sum.74 = f32[32,4,4,128]{3,0,2,1:T(8,128)S(1)} reduce(f32[2,32,4,4,128]{4,1,3,2,0:T(8,128)} %all-to-all-done.1, f32[]{:T(128)} %constant.7.clone.1), dimensions={0}, to_apply=%region_2.0 | reduce | flops 65536 | bytes 786436 | tf_op jit(solution)/shard_map/reduce_sum | solution.py:15
  28.4 2.9 %fusion.2 = f32[4]{0:T(128)S(1)} fusion(f32[32,4,4,128]{3,0,2,1:T(8,128)S(1)} %reduce_sum.74, f32[128,4,4,32]{0,3,2,1:T(8,128)} %fusion.8, f32[4,128,128]{2,1,0:T(8,128)} %param.21), kind=kOutput, calls=%fused_computation.4 | convolution fusion | flops 101187584 | bytes 786448 | tf_op jit(solution)/shard_map/cmer,cmes->mers/dot_general | solution.py:65
  31.4 5.3 %all-to-all-done = f32[2,128,2,4,128]{1,4,3,2,0:T(8,128)} async-done(((f32[2,128,2,4,128]{1,4,3,2,0:T(8,128)}), f32[2,128,2,4,128]{1,4,3,2,0:T(8,128)}, u32[]{:S(2)}, u32[]{:S(2)}) %all-to-all-start) | async-done | bytes 1048608 | tf_op jit(solution)/shard_map/all_to_all | solution.py:14
  36.6 2.2 %reduce_sum.72 = f32[128,2,4,128]{0,3,2,1:T(8,128)} reduce(f32[2,128,2,4,128]{1,4,3,2,0:T(8,128)} %all-to-all-done, f32[]{:T(128)} %constant.7.clone.1), dimensions={0}, to_apply=%region_0.0 | reduce | flops 131072 | bytes 1572868 | tf_op jit(solution)/shard_map/reduce_sum | solution.py:15
  38.8 0.0 copy-done.3
  38.8 2.4 %fusion.6 = f32[4]{0:T(128)S(1)} fusion(f32[128,2,4,128]{0,3,2,1:T(8,128)} %reduce_sum.72, f32[128,2,4,128]{0,3,2,1:T(8,128)S(1)} %fusion.3, f32[2,128,128]{2,1,0:T(8,128)S(1)} %copy-done.3), kind=kOutput, calls=%fused_computation.7 | convolution fusion | flops 201588736 | bytes 1179664 | tf_op jit(solution)/shard_map/fquy,fquh->quyh/dot_general | solution.py:53
  41.2 7.1 %all_to_all.22 = f32[4,1,4]{2,1,0:T(1,128)S(1)} all-to-all(f32[4,1,4]{2,1,0:T(1,128)S(1)} %broadcast_in_dim.4), channel_id=1, replica_groups=mesh['dp'=32,'expert'=2,'tensor'=2] {'expert','tensor'}, dimensions={0} | all-to-all | bytes 128 | tf_op jit(solution)/shard_map/all_to_all | solution.py:20
  48.3 0.0 copy-done.5
  48.3 0.2 convolution_bitcast_fusion.1
  48.5 0.6 broadcast_in_dim.5
  49.1 10.8 %all-to-all-start.3 = ((f32[32,1,64]{2,1,0:T(1,128)}), f32[32,1,64]{2,1,0:T(1,128)S(1)}, u32[]{:S(2)}, u32[]{:S(2)}) async-start(f32[32,1,64]{2,1,0:T(1,128)} %broadcast_in_dim.5), calls=%async_computation.3 | async-start | bytes 32768 | tf_op jit(solution)/shard_map/all_to_all | solution.py:20
  59.9 8.6 %all-to-all-done.3 = f32[32,1,64]{2,1,0:T(1,128)S(1)} async-done(((f32[32,1,64]{2,1,0:T(1,128)}), f32[32,1,64]{2,1,0:T(1,128)S(1)}, u32[]{:S(2)}, u32[]{:S(2)}) %all-to-all-start.3) | async-done | bytes 8224 | tf_op jit(solution)/shard_map/all_to_all | solution.py:20
  68.5 0.6 multiply_reduce_fusion.1
  69.8 0.0 copy-done.4
  69.8 0.6 multiply_reduce_fusion
  71.1 0.6 add_subtract_fusion
  (4 shorter events, 0.1 us)
Async XLA Ops:
  0.0 1.7 %copy-start = (bf16[4,4,64,1280]{3,2,1,0:T(8,128)(2,1)S(1)}, bf16[4,4,64,1280]{3,2,1,0:T(8,128)(2,1)}, u32[]{:S(2)}) copy-start(bf16[4,4,64,1280]{3,2,1,0:T(8,128)(2,1)} %param.16) | copy-start | bytes 7864324
  4.4 14.3 %all-to-all-start.1 = ((f32[2,32,4,4,128]{4,1,3,2,0:T(8,128)}), f32[2,32,4,4,128]{4,1,3,2,0:T(8,128)}, u32[]{:S(2)}, u32[]{:S(2)}) async-start(f32[2,32,4,4,128]{4,1,3,2,0:T(8,128)} %copy.31), calls=%async_computation.1 | async-start | bytes 1048576 | tf_op jit(solution)/shard_map/all_to_all | solution.py:14
  8.6 6.4 %copy-start.1 = (bf16[2,4,256,1792]{3,2,1,0:T(8,128)(2,1)S(1)}, bf16[2,4,256,1792]{3,2,1,0:T(8,128)(2,1)}, u32[]{:S(2)}) copy-start(bf16[2,4,256,1792]{3,2,1,0:T(8,128)(2,1)} %param.12) | copy-start | bytes 22020100
  8.6 6.4 %copy-start.2 = (bf16[2,1792,128]{2,1,0:T(8,128)(2,1)S(1)}, bf16[2,1792,128]{2,1,0:T(8,128)(2,1)}, u32[]{:S(2)}) copy-start(bf16[2,1792,128]{2,1,0:T(8,128)(2,1)} %param.14) | copy-start | bytes 2752516
  18.7 17.9 %all-to-all-start = ((f32[2,128,2,4,128]{1,4,3,2,0:T(8,128)}), f32[2,128,2,4,128]{1,4,3,2,0:T(8,128)}, u32[]{:S(2)}, u32[]{:S(2)}) async-start(f32[2,128,2,4,128]{1,4,3,2,0:T(8,128)} %bitcast.48), calls=%async_computation | async-start | bytes 2097152 | tf_op jit(solution)/shard_map/all_to_all | solution.py:14
  23.1 15.7 %copy-start.3 = (f32[2,128,128]{2,1,0:T(8,128)S(1)}, f32[2,128,128]{2,1,0:T(8,128)}, u32[]{:S(2)}) copy-start(f32[2,128,128]{2,1,0:T(8,128)} %param.20) | copy-start | bytes 393220
  27.3 21.0 %copy-start.5 = (s32[4]{0:T(128)S(1)}, s32[4]{0:T(128)}, u32[]{:S(2)}) copy-start(s32[4]{0:T(128)} %param.22) | copy-start | bytes 52
  27.3 42.5 %copy-start.4 = (f32[64]{0:T(128)S(1)}, f32[64]{0:T(128)}, u32[]{:S(2)}) copy-start(f32[64]{0:T(128)} %param.23) | copy-start | bytes 772
  49.1 19.4 %all-to-all-start.3 = ((f32[32,1,64]{2,1,0:T(1,128)}), f32[32,1,64]{2,1,0:T(1,128)S(1)}, u32[]{:S(2)}, u32[]{:S(2)}) async-start(f32[32,1,64]{2,1,0:T(1,128)} %broadcast_in_dim.5), calls=%async_computation.3 | async-start | bytes 32768 | tf_op jit(solution)/shard_map/all_to_all | solution.py:20
where the time goes:
time: 72.9 us; the launch traced here: 71.7 us
  matrix products  20.3 us (28%)
  starting transfers between devices  19.4 us (27%)
  waiting for transfers between devices  13.9 us (19%)
  blocking collectives  7.1 us (10%)
  other arithmetic  5.14 us (7%)
  local copies, waits for them, and re-layouts  4.37 us (6%)
  between operations  1.5 us (2%)
    all_to_all x1, starting transfers between devices, from_everyone(): lax.all_to_all(jnp.broadcast_to(array[None], (peers, *array.shape)), axis...  10.8 us
    all_to_all x2, starting transfers between devices, sum_at_owner(): lax.all_to_all(tiles, axis, split_axis=0, concat_axis=0, tiled=True)  8.64 us
    all_to_all x1, waiting for transfers between devices, from_everyone(): lax.all_to_all(jnp.broadcast_to(array[None], (peers, *array.shape)), axis...  8.61 us
    all_to_all x1, blocking collectives, from_everyone(): lax.all_to_all(jnp.broadcast_to(array[None], (peers, *array.shape)), axis...  7.1 us
    dot_general x1, matrix products, per_device(): jnp.einsum('lmtd,ldr->tlmr', dense_cot, dense_proj_out, preferred_element...  6.33 us
    all_to_all x2, waiting for transfers between devices, sum_at_owner(): lax.all_to_all(tiles, axis, split_axis=0, concat_axis=0, tiled=True)  5.26 us
    dot_general x1, matrix products, per_device(): jnp.einsum('mecd,dr->cmer', expert_cot, expert_proj_out, preferred_elemen...  4.17 us
    reduce_sum x2, other arithmetic, sum_at_owner(): return arrived.sum(axis=0)  3.27 us
  transfers between devices with their start and end apart: 3, of which 2 were waited for; matrix products, arithmetic and copies ran while one was open for 25% of the time, Pallas kernels for 0%

commit v1 on v0

v1 whole, which is shorter than its diff:
```python
import functools

import jax
import jax.numpy as jnp
from jax import lax
from jax.experimental import pallas as pl
from jax.experimental.pallas import tpu as pltpu
from jax.sharding import PartitionSpec as P

MESH = pl.DeviceIdType.MESH
F32 = jnp.float32
EXACT = lax.Precision.HIGHEST


def fold(product):
    rows, lanes = product.shape
    return jnp.sum(product.reshape(rows // 8, 8, lanes), axis=0)


def kernel(
    sizes,
    dense_act,
    dense_cot,
    dense_proj_in,
    dense_proj_out,
    expert_act,
    expert_cot,
    expert_proj_in,
    expert_proj_out,
    dense_valid,
    expert_valid,
    domain_ids,
    prior_mix,
    out,
    da,
    dc,
    pin,
    pout,
    ea,
    ec,
    epin,
    epout,
    dval,
    evalid,
    ids,
    prior,
    send,
    recv,
    wv,
    acc,
    row,
    rows,
    load_sem,
    send_sem,
    recv_sem,
    row_send_sem,
    row_recv_sem,
):
    n_dp, n_e, n_t = sizes
    devices = n_dp * n_e * n_t
    dp, ex, te = lax.axis_index("dp"), lax.axis_index("expert"), lax.axis_index("tensor")
    me = (dp * n_e + ex) * n_t + te
    layers, micro = dense_act.shape[0], dense_act.shape[1]
    half = dense_cot.shape[2]
    experts, slots = expert_cot.shape[1], expert_cot.shape[2]
    chunks = micro + layers * micro
    partner = {"tensor": 1 - te}

    def device(lid):
        return {
            "dp": lid // (n_e * n_t),
            "expert": (lid // n_t) % n_e,
            "tensor": lid % n_t,
        }

    loads = {}

    def load(name, src, dst):
        copy = pltpu.make_async_copy(src, dst, load_sem.at[len(loads)])
        loads[name] = copy

    other = pl.multiple_of((1 - te) * half, half)
    mine = pl.multiple_of(te * half, half)
    e_other = pl.multiple_of((1 - te) * slots, slots)
    e_mine = pl.multiple_of(te * slots, slots)
    load("epin", expert_proj_in, epin)
    for m in range(micro):
        load(("eao", m), expert_act.at[m, :, pl.ds(e_other, slots), :], ea.at[0, m])
    for l in range(layers):
        load(("pin", l), dense_proj_in.at[l], pin.at[l])
        for m in range(micro):
            load(("dao", l, m), dense_act.at[l, m, pl.ds(other, half), :], da.at[0, l, m])
    n_first = len(loads)
    load("ids", domain_ids, ids)
    load("prior", prior_mix, prior)
    load("epout", expert_proj_out, epout)
    load("evalid", expert_valid, evalid)
    load("dval", dense_valid, dval)
    for m in range(micro):
        load(("eam", m), expert_act.at[m, :, pl.ds(e_mine, slots), :], ea.at[1, m])
        load(("ec", m), expert_cot.at[m], ec.at[m])
    for l in range(layers):
        load(("pout", l), dense_proj_out.at[l], pout.at[l])
        for m in range(micro):
            load(("dam", l, m), dense_act.at[l, m, pl.ds(mine, half), :], da.at[1, l, m])
            load(("dc", l, m), dense_cot.at[l, m], dc.at[l, m])
    names = list(loads)
    for name in names[:n_first]:
        loads[name].start()

    barrier = pltpu.get_barrier_semaphore()

    def greet(k, carry):
        pl.semaphore_signal(
            barrier, inc=1, device_id=device((me + k) % devices), device_id_type=MESH
        )
        return carry

    lax.fori_loop(1, devices, greet, 0)

    def exchange(i):
        return pltpu.make_async_remote_copy(
            src_ref=send.at[i],
            dst_ref=recv.at[i],
            send_sem=send_sem.at[i],
            recv_sem=recv_sem.at[i],
            device_id=partner,
            device_id_type=MESH,
        )

    def project(block, weight):
        return jnp.dot(block, weight, preferred_element_type=F32)

    loads["epin"].wait()
    for m in range(micro):
        loads["eao", m].wait()
        block = ea[0, m].reshape(experts * slots, -1)
        send[m] = project(block, epin[...])
        if m == 0:
            pl.semaphore_wait(barrier, devices - 1)
        exchange(m).start()
        if m == 0:
            for name in names[n_first:]:
                loads[name].start()
    for l in range(layers):
        loads["pin", l].wait()
        for m in range(micro):
            loads["dao", l, m].wait()
            i = micro + l * micro + m
            send[i] = project(da[0, l, m], pin[l])
            exchange(i).start()

    for name in ("epout", "evalid", "dval"):
        loads[name].wait()
    for m in range(micro):
        loads["eam", m].wait()
        loads["ec", m].wait()
        u = project(ea[1, m].reshape(experts * slots, -1), epin[...])
        w = project(ec[m].reshape(experts * slots, -1), epout[...])
        parts = [
            lax.dot_general(
                w[e * slots : (e + 1) * slots],
                evalid[e],
                (((1,), (1,)), ((), ())),
                precision=EXACT,
                preferred_element_type=F32,
            )
            for e in range(experts)
        ]
        wv_i = jnp.concatenate(parts, axis=0)
        wv[m] = wv_i
        acc[m] = fold(u * wv_i)
    for l in range(layers):
        loads["pout", l].wait()
        for m in range(micro):
            loads["dam", l, m].wait()
            loads["dc", l, m].wait()
            i = micro + l * micro + m
            u = project(da[1, l, m], pin[l])
            w = project(dc[l, m], pout[l])
            wv_i = lax.dot_general(
                w, dval[l], (((1,), (1,)), ((), ())), precision=EXACT, preferred_element_type=F32
            )
            wv[i] = wv_i
            acc[m] += fold(u * wv_i)

    loads["ids"].wait()
    loads["prior"].wait()
    for i in range(chunks):
        m = i % micro
        exchange(i).wait_recv()
        acc[m] += fold(recv[i] * wv[i])

    lane = lax.broadcasted_iota(jnp.int32, (1, 128), 1)
    mine_row = jnp.zeros((1, 128), F32)
    for m in range(micro):
        s = jnp.sum(jnp.sum(acc[m], axis=0, keepdims=True), axis=1, keepdims=True)
        mine_row += jnp.where(lane == ids[m], s, 0.0)

    row[...] = mine_row
    rows[me] = mine_row

    def tell(k, carry):
        pltpu.make_async_remote_copy(
            src_ref=row,
            dst_ref=rows.at[me],
            send_sem=row_send_sem,
            recv_sem=row_recv_sem,
            device_id=device((me + k) % devices),
            device_id_type=MESH,
        ).start()
        return carry

    lax.fori_loop(1, devices, tell, 0)
    everyone = pltpu.make_async_remote_copy(
        src_ref=rows.at[pl.ds(0, devices - 1)],
        dst_ref=rows.at[pl.ds(0, devices - 1)],
        send_sem=row_send_sem,
        recv_sem=row_recv_sem,
        device_id=partner,
        device_id_type=MESH,
    )
    everyone.wait_recv()
    total = jnp.sum(rows[...], axis=0)

    domains = prior_mix.shape[0]
    total = total[:, :domains]
    mix = prior[...].reshape(1, domains)
    spread = jnp.sqrt(jnp.sum(total * total, axis=1, keepdims=True) / domains + 1e-06)
    z = total / spread
    mass = jnp.sum(mix * jnp.exp(0.5 * z), axis=1, keepdims=True)
    result = jnp.log(mix) + 0.5 * z - jnp.log(mass)
    share = domains // n_dp
    place = lax.broadcasted_iota(jnp.int32, (1, domains), 1)
    for j in range(share):
        out[j] = jnp.sum(jnp.where(place == dp * share + j, result, 0.0))

    everyone.wait_send()
    for i in range(chunks):
        exchange(i).wait_send()


def per_device(*args):
    (
        dense_act,
        dense_cot,
        dense_proj_in,
        dense_proj_out,
        expert_act,
        expert_cot,
        expert_proj_in,
        expert_proj_out,
        dense_valid,
        expert_valid,
        domain_ids,
        prior_mix,
    ) = args
    sizes = tuple(lax.axis_size(name) for name in ("dp", "expert", "tensor"))
    devices = sizes[0] * sizes[1] * sizes[2]
    layers, micro, tokens, feat = dense_act.shape
    half, width = dense_cot.shape[2:]
    experts, caps, hidden = expert_act.shape[1:]
    slots = expert_cot.shape[2]
    rank = dense_proj_in.shape[2]
    bf = dense_act.dtype
    chunks = micro + layers * micro
    n_loads = 1 + micro + layers * (1 + micro) + 5 + 2 * micro + layers * (1 + 2 * micro)
    return pl.pallas_call(
        functools.partial(kernel, sizes),
        out_shape=jax.ShapeDtypeStruct((prior_mix.shape[0] // sizes[0],), F32),
        in_specs=[pl.BlockSpec(memory_space=pl.ANY)] * len(args),
        out_specs=pl.BlockSpec(memory_space=pltpu.SMEM),
        scratch_shapes=[
            pltpu.VMEM((2, layers, micro, half, feat), bf),
            pltpu.VMEM((layers, micro, half, width), bf),
            pltpu.VMEM((layers, feat, rank), bf),
            pltpu.VMEM((layers, width, rank), bf),
            pltpu.VMEM((2, micro, experts, slots, hidden), bf),
            pltpu.VMEM((micro, experts, slots, width), bf),
            pltpu.VMEM((hidden, rank), bf),
            pltpu.VMEM((width, rank), bf),
            pltpu.VMEM(dense_valid.shape, F32),
            pltpu.VMEM(expert_valid.shape, F32),
            pltpu.SMEM(domain_ids.shape, jnp.int32),
            pltpu.VMEM(prior_mix.shape, F32),
            pltpu.VMEM((chunks, half, rank), F32),
            pltpu.VMEM((chunks, half, rank), F32),
            pltpu.VMEM((chunks, half, rank), F32),
            pltpu.VMEM((micro, 8, rank), F32),
            pltpu.VMEM((1, 128), F32),
            pltpu.VMEM((devices, 1, 128), F32),
            pltpu.SemaphoreType.DMA((n_loads,)),
            pltpu.SemaphoreType.DMA((chunks,)),
            pltpu.SemaphoreType.DMA((chunks,)),
            pltpu.SemaphoreType.DMA,
            pltpu.SemaphoreType.DMA,
        ],
        compiler_params=pltpu.CompilerParams(
            collective_id=0, has_side_effects=True, vmem_limit_bytes=60 << 20
        ),
        name="align",
    )(*args)


def solution(mesh):
    placed = (
        P(None, "dp", "expert", "tensor"),
        P(None, "dp", ("expert", "tensor"), None),
        P(None, "tensor", None),
        P(),
        P("dp", "expert", None, "tensor"),
        P("dp", "expert", "tensor", None),
        P("tensor", None),
        P(),
        P(),
        P("expert", None, None),
        P("dp"),
        P(),
    )
    return jax.shard_map(per_device, mesh=mesh, in_specs=placed, out_specs=P("dp"), check_vma=False)
```

time: 72.9 us -> 40.8 us (0.56); the launches traced: 71.7 us -> 40.7 us
  Pallas kernels: 0 us -> 39.5 us
  matrix products: 20.3 us -> 0 us
  starting transfers between devices: 19.4 us -> 0 us
  waiting for transfers between devices: 13.9 us -> 0 us
  blocking collectives: 7.1 us -> 0 us
  other arithmetic: 5.14 us -> 0 us
  local copies, waits for them, and re-layouts: 4.37 us -> 1.19 us
  between operations: 1.5 us -> 0.01 us
    pallas_call x0 -> x1, Pallas kernels: none -> 39.5 us  [per_device(): pl.pallas_call(functools.partial(kernel, sizes), out_shape=jax.ShapeDtype...]
    dot_general x7 -> x0, matrix products: 20.3 us -> none  [the longest x1 6.33 us: per_device(): jnp.einsum('lmtd,ldr->tlmr', dense_cot, dense_proj_out, preferred_element...]
    all_to_all x3 -> x0, starting transfers between devices: 19.4 us -> none  [the longest x1 10.8 us: from_everyone(): lax.all_to_all(jnp.broadcast_to(array[None], (peers, *array.shape)), axis...]
    all_to_all x3 -> x0, waiting for transfers between devices: 13.9 us -> none  [the longest x1 8.61 us: from_everyone(): lax.all_to_all(jnp.broadcast_to(array[None], (peers, *array.shape)), axis...]
    all_to_all x1 -> x0, blocking collectives: 7.1 us -> none  [from_everyone(): lax.all_to_all(jnp.broadcast_to(array[None], (peers, *array.shape)), axis...]
    reduce_sum x6 -> x0, other arithmetic: 4.53 us -> none  [the longest x2 3.27 us: sum_at_owner(): return arrived.sum(axis=0)]
    reshape x2 -> x0, local copies, waits for them, and re-layouts: 1.98 us -> none  [cut_along(): return jnp.moveaxis(array.reshape(*before, peers, -1, *after), dim, 0)]
    unnamed x12 -> x1, local copies, waits for them, and re-layouts: 1.77 us -> 1.19 us
  transfers between devices with their start and end apart: 3 -> 0, of which waited for: 2 -> 0; matrix products, arithmetic and copies ran while one was open for 25% -> 0% of each run, Pallas kernels for 0% -> 0%
where the time goes in v1:
time: 40.8 us; the launch traced here: 40.7 us
  Pallas kernels  39.5 us (97%)
  local copies, waits for them, and re-layouts  1.19 us (3%)
    pallas_call x1, Pallas kernels, per_device(): pl.pallas_call(functools.partial(kernel, sizes), out_shape=jax.ShapeDtype...  39.5 us
    unnamed x1, local copies, waits for them, and re-layouts  1.19 us

profile of v1, /device:TPU:1, one launch (start us, length us, event | category | flops | bytes accessed | tf_op | source)
XLA Modules:
  0.0 40.7 jit_solution(17902088050094876723)
XLA Ops:
  0.0 39.5 %align.1 = f32[2]{0:T(128)} custom-call(bf16[2,4,256,1792]{3,2,1,0:T(8,128)(2,1)} %dense_act.1, bf16[2,4,128,3584]{3,2,1,0:T(8,128)(2,1)} %dense_cot.1, bf16[2,1792,128]{2,1,0:T(8,128)(2,1)} %dense_proj_in.1, bf16[2,3584,128]{2,1,0:T(8,128)(2,1)} %dense_proj_out.1, bf16[4,4,64,1280]{3,2,1,0:T(8,128)(2,1)} %expert_act.1, bf16[4,4,32,3584]{3,2,1,0:T(8,128)(2,1)} %expert_cot.1, ...), custom_call_target="tpu_custom_call" | custom-call | tf_op jit(solution)/shard_map/align/pallas_call | solution.py:268
  39.5 1.2 %copy.14 = f32[2]{0:T(128)} copy(f32[2]{0:T(128)} %align.1) | data formatting | bytes 16

commit v2 on v1

--- a/solution.py
+++ b/solution.py
@@ -50,6 +50,7 @@
     acc,
     row,
     rows,
+    here,
     load_sem,
     send_sem,
     recv_sem,
@@ -66,12 +67,30 @@
     chunks = micro + layers * micro
     partner = {"tensor": 1 - te}
 
-    def device(lid):
-        return {
-            "dp": lid // (n_e * n_t),
-            "expert": (lid // n_t) % n_e,
-            "tensor": lid % n_t,
-        }
+    ring = 4
+    x, y, z = (dp % 2) * 2 + te, (dp // 2) % ring, dp // (2 * ring)
+
+    def away(offset):
+        dc, dx, dy, dz = offset
+        cc = (ex + dc) % n_e
+        xx, yy, zz = (x + dx) % ring, (y + dy) % ring, (z + dz) % ring
+        return (((zz * ring + yy) * 2 + xx // n_t) * n_e + cc) * n_t + xx % n_t
+
+    around = [(1, 0, 0, 0)]
+    for axis in (1, 2, 3):
+        for step in (1, ring - 1):
+            around.append(tuple(step if k == axis else 0 for k in range(4)))
+    lines = {
+        axis: [tuple(step if k == axis else 0 for k in range(4)) for step in range(1, ring)]
+        for axis in (1, 2, 3)
+    }
+    rounds = [around, lines[1], lines[2], around[:1]]
+
+    def hello(semaphore, offsets):
+        for offset in offsets:
+            pl.semaphore_signal(
+                semaphore, inc=1, device_id=away(offset), device_id_type=pl.DeviceIdType.LOGICAL
+            )
 
     loads = {}
 
@@ -109,14 +128,7 @@
         loads[name].start()
 
     barrier = pltpu.get_barrier_semaphore()
-
-    def greet(k, carry):
-        pl.semaphore_signal(
-            barrier, inc=1, device_id=device((me + k) % devices), device_id_type=MESH
-        )
-        return carry
-
-    lax.fori_loop(1, devices, greet, 0)
+    hello(barrier, around)
 
     def exchange(i):
         return pltpu.make_async_remote_copy(
@@ -137,7 +149,8 @@
         block = ea[0, m].reshape(experts * slots, -1)
         send[m] = project(block, epin[...])
         if m == 0:
-            pl.semaphore_wait(barrier, devices - 1)
+            pl.semaphore_wait(barrier, len(around))
+            hello(here.at[0], rounds[0])
         exchange(m).start()
         if m == 0:
             for name in names[n_first:]:
@@ -153,6 +166,9 @@
     for name in ("epout", "evalid", "dval"):
         loads[name].wait()
     for m in range(micro):
+        pl.semaphore_wait(here.at[m], len(rounds[m]))
+        if m + 1 < len(rounds):
+            hello(here.at[m + 1], rounds[m + 1])
         loads["eam", m].wait()
         loads["ec", m].wait()
         u = project(ea[1, m].reshape(experts * slots, -1), epin[...])
@@ -200,18 +216,24 @@
     row[...] = mine_row
     rows[me] = mine_row
 
-    def tell(k, carry):
+    hops = lambda offset: sum(min(d, n - d) for d, n in zip(offset, (2, ring, ring, ring)))
+    offsets = [
+        (dc, dx, dy, dz)
+        for dc in range(n_e)
+        for dx in range(ring)
+        for dy in range(ring)
+        for dz in range(ring)
+    ][1:]
+    offsets.sort(key=hops, reverse=True)
+    for offset in offsets:
         pltpu.make_async_remote_copy(
             src_ref=row,
             dst_ref=rows.at[me],
             send_sem=row_send_sem,
             recv_sem=row_recv_sem,
-            device_id=device((me + k) % devices),
-            device_id_type=MESH,
+            device_id=away(offset),
+            device_id_type=pl.DeviceIdType.LOGICAL,
         ).start()
-        return carry
-
-    lax.fori_loop(1, devices, tell, 0)
     everyone = pltpu.make_async_remote_copy(
         src_ref=rows.at[pl.ds(0, devices - 1)],
         dst_ref=rows.at[pl.ds(0, devices - 1)],
@@ -289,6 +311,7 @@
             pltpu.VMEM((micro, 8, rank), F32),
             pltpu.VMEM((1, 128), F32),
             pltpu.VMEM((devices, 1, 128), F32),
+            pltpu.SemaphoreType.REGULAR((4,)),
             pltpu.SemaphoreType.DMA((n_loads,)),
             pltpu.SemaphoreType.DMA((chunks,)),
             pltpu.SemaphoreType.DMA((chunks,)),

time: 40.8 us -> 34.7 us (0.85)
  Pallas kernels: 39.5 us -> 33.4 us
    pallas_call x1, Pallas kernels: 39.5 us -> 33.4 us  [per_device(): pl.pallas_call(functools.partial(kernel, sizes), out_shape=jax.ShapeDtype...]
where the time goes in v2:
time: 34.7 us; the launch traced here: 34.6 us
  Pallas kernels  33.4 us (96%)
  local copies, waits for them, and re-layouts  1.19 us (3%)
    pallas_call x1, Pallas kernels, per_device(): pl.pallas_call(functools.partial(kernel, sizes), out_shape=jax.ShapeDtype...  33.4 us
    unnamed x1, local copies, waits for them, and re-layouts  1.19 us

profile of v2, /device:TPU:1, one launch (start us, length us, event | category | flops | bytes accessed | tf_op | source)
XLA Modules:
  0.0 34.6 jit_solution(12545330653607969504)
XLA Ops:
  0.0 33.4 %align.1 = f32[2]{0:T(128)} custom-call(bf16[2,4,256,1792]{3,2,1,0:T(8,128)(2,1)} %dense_act.1, bf16[2,4,128,3584]{3,2,1,0:T(8,128)(2,1)} %dense_cot.1, bf16[2,1792,128]{2,1,0:T(8,128)(2,1)} %dense_proj_in.1, bf16[2,3584,128]{2,1,0:T(8,128)(2,1)} %dense_proj_out.1, bf16[4,4,64,1280]{3,2,1,0:T(8,128)(2,1)} %expert_act.1, bf16[4,4,32,3584]{3,2,1,0:T(8,128)(2,1)} %expert_cot.1, ...), custom_call_target="tpu_custom_call" | custom-call | tf_op jit(solution)/shard_map/align/pallas_call | solution.py:290
  33.4 1.2 %copy.14 = f32[2]{0:T(128)} copy(f32[2]{0:T(128)} %align.1) | data formatting | bytes 16

commit v3 on v2

--- a/solution.py
+++ b/solution.py
@@ -92,50 +92,47 @@
                 semaphore, inc=1, device_id=away(offset), device_id_type=pl.DeviceIdType.LOGICAL
             )
 
-    loads = {}
-
-    def load(name, src, dst):
-        copy = pltpu.make_async_copy(src, dst, load_sem.at[len(loads)])
-        loads[name] = copy
-
     other = pl.multiple_of((1 - te) * half, half)
     mine = pl.multiple_of(te * half, half)
     e_other = pl.multiple_of((1 - te) * slots, slots)
     e_mine = pl.multiple_of(te * slots, slots)
-    load("epin", expert_proj_in, epin)
-    for m in range(micro):
-        load(("eao", m), expert_act.at[m, :, pl.ds(e_other, slots), :], ea.at[0, m])
-    for l in range(layers):
-        load(("pin", l), dense_proj_in.at[l], pin.at[l])
-        for m in range(micro):
-            load(("dao", l, m), dense_act.at[l, m, pl.ds(other, half), :], da.at[0, l, m])
-    n_first = len(loads)
-    load("ids", domain_ids, ids)
-    load("prior", prior_mix, prior)
-    load("epout", expert_proj_out, epout)
-    load("evalid", expert_valid, evalid)
-    load("dval", dense_valid, dval)
-    for m in range(micro):
-        load(("eam", m), expert_act.at[m, :, pl.ds(e_mine, slots), :], ea.at[1, m])
-        load(("ec", m), expert_cot.at[m], ec.at[m])
-    for l in range(layers):
-        load(("pout", l), dense_proj_out.at[l], pout.at[l])
-        for m in range(micro):
-            load(("dam", l, m), dense_act.at[l, m, pl.ds(mine, half), :], da.at[1, l, m])
-            load(("dc", l, m), dense_cot.at[l, m], dc.at[l, m])
-    names = list(loads)
-    for name in names[:n_first]:
+    rest = pl.ds(1, micro - 1)
+    plan = {
+        "epin": (expert_proj_in, epin),
+        "eao0": (expert_act.at[0, :, pl.ds(e_other, slots), :], ea.at[0, 0]),
+        "eao": (expert_act.at[rest, :, pl.ds(e_other, slots), :], ea.at[0, rest]),
+        "pin": (dense_proj_in, pin),
+        ("dao", 0): (dense_act.at[0, :, pl.ds(other, half), :], da.at[0, 0]),
+        ("dao", 1): (dense_act.at[1, :, pl.ds(other, half), :], da.at[0, 1]),
+        "epout": (expert_proj_out, epout),
+        "eam": (expert_act.at[:, :, pl.ds(e_mine, slots), :], ea.at[1]),
+        "ec": (expert_cot, ec),
+        "evalid": (expert_valid, evalid),
+        "dval": (dense_valid, dval),
+        "ids": (domain_ids, ids),
+        "prior": (prior_mix, prior),
+        "pout": (dense_proj_out, pout),
+        ("dam", 0): (dense_act.at[0, :, pl.ds(mine, half), :], da.at[1, 0]),
+        ("dc", 0): (dense_cot.at[0], dc.at[0]),
+        ("dam", 1): (dense_act.at[1, :, pl.ds(mine, half), :], da.at[1, 1]),
+        ("dc", 1): (dense_cot.at[1], dc.at[1]),
+    }
+    names = list(plan)
+    loads = {
+        name: pltpu.make_async_copy(*plan[name], load_sem.at[k]) for k, name in enumerate(names)
+    }
+    for name in names[:6]:
         loads[name].start()
 
     barrier = pltpu.get_barrier_semaphore()
     hello(barrier, around)
 
-    def exchange(i):
+    def exchange(part, group):
         return pltpu.make_async_remote_copy(
-            src_ref=send.at[i],
-            dst_ref=recv.at[i],
-            send_sem=send_sem.at[i],
-            recv_sem=recv_sem.at[i],
+            src_ref=send.at[part],
+            dst_ref=recv.at[part],
+            send_sem=send_sem,
+            recv_sem=recv_sem.at[group],
             device_id=partner,
             device_id_type=MESH,
         )
@@ -144,33 +141,34 @@
         return jnp.dot(block, weight, preferred_element_type=F32)
 
     loads["epin"].wait()
-    for m in range(micro):
-        loads["eao", m].wait()
-        block = ea[0, m].reshape(experts * slots, -1)
-        send[m] = project(block, epin[...])
-        if m == 0:
-            pl.semaphore_wait(barrier, len(around))
-            hello(here.at[0], rounds[0])
-        exchange(m).start()
-        if m == 0:
-            for name in names[n_first:]:
-                loads[name].start()
+    loads["eao0"].wait()
+    head, tail = pl.ds(0, slots), pl.ds(slots, (experts - 1) * slots)
+    send[0, head] = project(ea[0, 0, 0], epin[...])
+    pl.semaphore_wait(barrier, len(around))
+    exchange((0, head), 0).start()
+    for name in names[6:]:
+        loads[name].start()
+    hello(here.at[0], rounds[0])
+    send[0, tail] = project(ea[0, 0, 1:].reshape((experts - 1) * slots, -1), epin[...])
+    exchange((0, tail), 0).start()
+    loads["eao"].wait()
+    for m in range(1, micro):
+        send[m] = project(ea[0, m].reshape(experts * slots, -1), epin[...])
+        exchange(m, 0).start()
+    loads["pin"].wait()
     for l in range(layers):
-        loads["pin", l].wait()
+        loads["dao", l].wait()
         for m in range(micro):
-            loads["dao", l, m].wait()
             i = micro + l * micro + m
             send[i] = project(da[0, l, m], pin[l])
-            exchange(i).start()
-
-    for name in ("epout", "evalid", "dval"):
+            exchange(i, i // (chunks - 1)).start()
+
+    for name in ("epout", "evalid", "dval", "eam", "ec"):
         loads[name].wait()
     for m in range(micro):
         pl.semaphore_wait(here.at[m], len(rounds[m]))
         if m + 1 < len(rounds):
             hello(here.at[m + 1], rounds[m + 1])
-        loads["eam", m].wait()
-        loads["ec", m].wait()
         u = project(ea[1, m].reshape(experts * slots, -1), epin[...])
         w = project(ec[m].reshape(experts * slots, -1), epout[...])
         parts = [
@@ -186,11 +184,11 @@
         wv_i = jnp.concatenate(parts, axis=0)
         wv[m] = wv_i
         acc[m] = fold(u * wv_i)
+    loads["pout"].wait()
     for l in range(layers):
-        loads["pout", l].wait()
+        loads["dam", l].wait()
+        loads["dc", l].wait()
         for m in range(micro):
-            loads["dam", l, m].wait()
-            loads["dc", l, m].wait()
             i = micro + l * micro + m
             u = project(da[1, l, m], pin[l])
             w = project(dc[l, m], pout[l])
@@ -199,18 +197,31 @@
             )
             wv[i] = wv_i
             acc[m] += fold(u * wv_i)
-
     loads["ids"].wait()
     loads["prior"].wait()
-    for i in range(chunks):
-        m = i % micro
-        exchange(i).wait_recv()
-        acc[m] += fold(recv[i] * wv[i])
-
+    domains = prior_mix.shape[0]
+    share = domains // n_dp
+    mix = prior[...].reshape(1, domains)
+    log_mix = jnp.log(mix)
+    place = lax.broadcasted_iota(jnp.int32, (1, domains), 1)
     lane = lax.broadcasted_iota(jnp.int32, (1, 128), 1)
+
+    def own(values, j):
+        return jnp.sum(jnp.where(place == dp * share + j, values, 0.0), axis=1, keepdims=True)
+
+    early = pl.ds(0, chunks - 1)
+    exchange(early, 0).wait_recv()
+    sums = []
+    for m in range(micro):
+        s = acc[m]
+        for i in range(m, chunks - 1, micro):
+            s += fold(recv[i] * wv[i])
+        sums.append(s)
+    exchange(chunks - 1, 1).wait_recv()
+    sums[micro - 1] += fold(recv[chunks - 1] * wv[chunks - 1])
     mine_row = jnp.zeros((1, 128), F32)
     for m in range(micro):
-        s = jnp.sum(jnp.sum(acc[m], axis=0, keepdims=True), axis=1, keepdims=True)
+        s = jnp.sum(jnp.sum(sums[m], axis=0, keepdims=True), axis=1, keepdims=True)
         mine_row += jnp.where(lane == ids[m], s, 0.0)
 
     row[...] = mine_row
@@ -225,13 +236,18 @@
         for dz in range(ring)
     ][1:]
     offsets.sort(key=hops, reverse=True)
-    for offset in offsets:
+    targets = [away(offset) for offset in offsets]
+    for k, first in enumerate((0, n_t)):
+        first = jnp.where(me == first, targets[k], first)
+        targets[k + 1 :] = [jnp.where(t == first, targets[k], t) for t in targets[k + 1 :]]
+        targets[k] = first
+    for target in targets:
         pltpu.make_async_remote_copy(
             src_ref=row,
             dst_ref=rows.at[me],
             send_sem=row_send_sem,
             recv_sem=row_recv_sem,
-            device_id=away(offset),
+            device_id=target,
             device_id_type=pl.DeviceIdType.LOGICAL,
         ).start()
     everyone = pltpu.make_async_remote_copy(
@@ -243,23 +259,18 @@
         device_id_type=MESH,
     )
     everyone.wait_recv()
-    total = jnp.sum(rows[...], axis=0)
-
-    domains = prior_mix.shape[0]
-    total = total[:, :domains]
-    mix = prior[...].reshape(1, domains)
+    total = jnp.sum(rows.reshape(devices, 128)[...], axis=0, keepdims=True)[:, :domains]
     spread = jnp.sqrt(jnp.sum(total * total, axis=1, keepdims=True) / domains + 1e-06)
-    z = total / spread
-    mass = jnp.sum(mix * jnp.exp(0.5 * z), axis=1, keepdims=True)
-    result = jnp.log(mix) + 0.5 * z - jnp.log(mass)
-    share = domains // n_dp
-    place = lax.broadcasted_iota(jnp.int32, (1, domains), 1)
+    mass = jnp.sum(mix * jnp.exp(0.5 * (total / spread)), axis=1, keepdims=True)
+    common = jnp.log(mass)
+    answer = jnp.zeros((1, 128), F32)
     for j in range(share):
-        out[j] = jnp.sum(jnp.where(place == dp * share + j, result, 0.0))
+        picked = own(log_mix, j) + 0.5 * (own(total, j) / spread) - common
+        answer = jnp.where(lane == j, picked, answer)
+    out[...] = answer[:, :share].reshape(share)
 
     everyone.wait_send()
-    for i in range(chunks):
-        exchange(i).wait_send()
+    exchange(pl.ds(0, chunks), 0).wait_send()
 
 
 def per_device(*args):
@@ -286,12 +297,12 @@
     rank = dense_proj_in.shape[2]
     bf = dense_act.dtype
     chunks = micro + layers * micro
-    n_loads = 1 + micro + layers * (1 + micro) + 5 + 2 * micro + layers * (1 + 2 * micro)
+    n_loads = 18
     return pl.pallas_call(
         functools.partial(kernel, sizes),
         out_shape=jax.ShapeDtypeStruct((prior_mix.shape[0] // sizes[0],), F32),
         in_specs=[pl.BlockSpec(memory_space=pl.ANY)] * len(args),
-        out_specs=pl.BlockSpec(memory_space=pltpu.SMEM),
+        out_specs=pl.BlockSpec(memory_space=pltpu.VMEM),
         scratch_shapes=[
             pltpu.VMEM((2, layers, micro, half, feat), bf),
             pltpu.VMEM((layers, micro, half, width), bf),
@@ -313,13 +324,13 @@
             pltpu.VMEM((devices, 1, 128), F32),
             pltpu.SemaphoreType.REGULAR((4,)),
             pltpu.SemaphoreType.DMA((n_loads,)),
-            pltpu.SemaphoreType.DMA((chunks,)),
-            pltpu.SemaphoreType.DMA((chunks,)),
+            pltpu.SemaphoreType.DMA,
+            pltpu.SemaphoreType.DMA((2,)),
             pltpu.SemaphoreType.DMA,
             pltpu.SemaphoreType.DMA,
         ],
         compiler_params=pltpu.CompilerParams(
-            collective_id=0, has_side_effects=True, vmem_limit_bytes=60 << 20
+            collective_id=0, has_side_effects=True, vmem_limit_bytes=56551424
         ),
         name="align",
     )(*args)

time: 34.7 us -> 32.8 us (0.945)
  Pallas kernels: 33.4 us -> 32.1 us
  local copies, waits for them, and re-layouts: 1.19 us -> 0.51 us
    pallas_call x1, Pallas kernels: 33.4 us -> 32.1 us  [per_device(): pl.pallas_call(functools.partial(kernel, sizes), out_shape=jax.ShapeDtype...]
    unnamed x1, local copies, waits for them, and re-layouts: 1.19 us -> 0.51 us
where the time goes in v3:
time: 32.8 us; the launch traced here: 32.7 us
  Pallas kernels  32.1 us (98%)
  local copies, waits for them, and re-layouts  0.51 us (2%)
    pallas_call x1, Pallas kernels, per_device(): pl.pallas_call(functools.partial(kernel, sizes), out_shape=jax.ShapeDtype...  32.1 us

profile of v3, /device:TPU:1, one launch (start us, length us, event | category | flops | bytes accessed | tf_op | source)
XLA Modules:
  0.0 32.7 jit_solution(17640075802135487040)
XLA Ops:
  0.0 32.1 %align.1 = f32[2]{0:T(128)S(1)} custom-call(bf16[2,4,256,1792]{3,2,1,0:T(8,128)(2,1)} %dense_act.1, bf16[2,4,128,3584]{3,2,1,0:T(8,128)(2,1)} %dense_cot.1, bf16[2,1792,128]{2,1,0:T(8,128)(2,1)} %dense_proj_in.1, bf16[2,3584,128]{2,1,0:T(8,128)(2,1)} %dense_proj_out.1, bf16[4,4,64,1280]{3,2,1,0:T(8,128)(2,1)} %expert_act.1, ...), custom_call_target="tpu_custom_call" | custom-call | tf_op jit(solution)/shard_map/align/pallas_call | solution.py:301
  32.1 0.5 %copy.14 = f32[2]{0:T(128)} copy(f32[2]{0:T(128)S(1)} %align.1) | data formatting | bytes 16

commit v4 on v3

--- a/solution.py
+++ b/solution.py
@@ -9,6 +9,9 @@
 
 MESH = pl.DeviceIdType.MESH
 F32 = jnp.float32
+HOLD = 8
+KEEP = 6
+SPARE = 3
 EXACT = lax.Precision.HIGHEST
 
 
@@ -50,6 +53,9 @@
     acc,
     row,
     rows,
+    relay_a,
+    relay_b,
+    relay_sem,
     here,
     load_sem,
     send_sem,
@@ -70,27 +76,81 @@
     ring = 4
     x, y, z = (dp % 2) * 2 + te, (dp // 2) % ring, dp // (2 * ring)
 
+    last = ring - 1
+
+    def number(cc, xx, yy, zz):
+        return (((zz * ring + yy) * 2 + xx // n_t) * n_e + cc) * n_t + xx % n_t
+
     def away(offset):
         dc, dx, dy, dz = offset
-        cc = (ex + dc) % n_e
-        xx, yy, zz = (x + dx) % ring, (y + dy) % ring, (z + dz) % ring
-        return (((zz * ring + yy) * 2 + xx // n_t) * n_e + cc) * n_t + xx % n_t
-
-    around = [(1, 0, 0, 0)]
-    for axis in (1, 2, 3):
-        for step in (1, ring - 1):
-            around.append(tuple(step if k == axis else 0 for k in range(4)))
-    lines = {
-        axis: [tuple(step if k == axis else 0 for k in range(4)) for step in range(1, ring)]
-        for axis in (1, 2, 3)
+        return number((ex + dc) % n_e, (x + dx) % ring, (y + dy) % ring, (z + dz) % ring)
+
+    def signal(semaphore, target):
+        pl.semaphore_signal(
+            semaphore, inc=1, device_id=target, device_id_type=pl.DeviceIdType.LOGICAL
+        )
+
+    def signal_if(condition, semaphore, target):
+        @pl.when(condition)
+        def _():
+            signal(semaphore, target)
+
+    age = y + 2 * z
+    mate, sibling, across = number(ex, x + 1 - 2 * te, y, z), number(1 - ex, x, y, z), number(ex, last - x, y, z)
+    mirror = number(ex, x, last - y, last - z)
+    up_y, down_y = number(ex, x, (y + 1) % ring, z), number(ex, x, (y + last) % ring, z)
+    up_z, down_z = number(ex, x, y, (z + 1) % ring), number(ex, x, y, (z + last) % ring)
+    giver2, giver1 = age >= 8, age >= 6
+    helper2, helper1 = age <= 1, age <= 3
+
+    def hello(k):
+        if k == 0:
+            semaphore = pltpu.get_barrier_semaphore()
+            signal(semaphore, mate)
+            signal(semaphore, sibling)
+            signal_if(x < n_t, semaphore, across)
+            signal_if(helper1, semaphore, mirror)
+        else:
+            semaphore = here.at[k - 1]
+        if k == 1:
+            signal_if(x >= n_t, semaphore, across)
+        if k in (2, 3):
+            for target in (mate, sibling, across):
+                signal(semaphore, target)
+        if k in (0, 2, 3):
+            signal_if(y < last, semaphore, up_y)
+            signal_if(z < last, semaphore, up_z)
+        if k in (1, 2, 3):
+            signal_if(y > 0, semaphore, down_y)
+            signal_if(z > 0, semaphore, down_z)
+        if k in (4, 5):
+            for step in range(1, ring):
+                signal(semaphore, away((0, step, 0, 0) if k == 4 else (0, 0, step, 0)))
+        if k == 6:
+            signal(semaphore, sibling)
+
+    from_below = (y + last) // ring + (z + last) // ring
+    from_above = 2 - y // last - z // last
+    heard = {
+        0: 2 + from_below + x // n_t + age // 6,
+        1: from_above + 1 - x // n_t,
+        2: 3 + from_below + from_above,
+        3: 3 + from_below + from_above,
+        4: ring - 1,
+        5: ring - 1,
+        6: 1,
     }
-    rounds = [around, lines[1], lines[2], around[:1]]
-
-    def hello(semaphore, offsets):
-        for offset in offsets:
-            pl.semaphore_signal(
-                semaphore, inc=1, device_id=away(offset), device_id_type=pl.DeviceIdType.LOGICAL
-            )
+
+    def listen(k):
+        semaphore = pltpu.get_barrier_semaphore() if k == 0 else here.at[k - 1]
+        if k == 1:
+
+            @pl.when(heard[k] > 0)
+            def _():
+                pl.semaphore_wait(semaphore, heard[k])
+
+        else:
+            pl.semaphore_wait(semaphore, heard[k])
 
     other = pl.multiple_of((1 - te) * half, half)
     mine = pl.multiple_of(te * half, half)
@@ -124,8 +184,7 @@
     for name in names[:6]:
         loads[name].start()
 
-    barrier = pltpu.get_barrier_semaphore()
-    hello(barrier, around)
+    hello(0)
 
     def exchange(part, group):
         return pltpu.make_async_remote_copy(
@@ -140,35 +199,108 @@
     def project(block, weight):
         return jnp.dot(block, weight, preferred_element_type=F32)
 
+    halves = (pl.ds(0, half // 2), pl.ds(half // 2, half // 2))
+
+    def hop(source, target, sent, arrived, device):
+        return pltpu.make_async_remote_copy(
+            src_ref=source,
+            dst_ref=target,
+            send_sem=sent,
+            recv_sem=arrived,
+            device_id=device,
+            device_id_type=pl.DeviceIdType.LOGICAL,
+        )
+
+    def give(k):
+        return hop(send.at[SPARE, halves[k]], relay_a.at[k], send_sem, relay_sem.at[0, k], mirror)
+
+    def pass_on(k):
+        return hop(relay_a.at[k], relay_b.at[k], relay_sem.at[1, k], relay_sem.at[2, k], mate)
+
+    def deliver(k):
+        return hop(
+            relay_b.at[k], recv.at[SPARE, halves[k]], relay_sem.at[3, k], recv_sem.at[0], mirror
+        )
+
     loads["epin"].wait()
     loads["eao0"].wait()
     head, tail = pl.ds(0, slots), pl.ds(slots, (experts - 1) * slots)
     send[0, head] = project(ea[0, 0, 0], epin[...])
-    pl.semaphore_wait(barrier, len(around))
+    listen(0)
     exchange((0, head), 0).start()
     for name in names[6:]:
         loads[name].start()
-    hello(here.at[0], rounds[0])
+    hello(1)
     send[0, tail] = project(ea[0, 0, 1:].reshape((experts - 1) * slots, -1), epin[...])
     exchange((0, tail), 0).start()
     loads["eao"].wait()
+    send[SPARE] = project(ea[0, SPARE].reshape(experts * slots, -1), epin[...])
+    for k, giver in enumerate((giver1, giver2)):
+
+        @pl.when(giver)
+        def _():
+            give(k).start()
+
+        @pl.when(jnp.logical_not(giver))
+        def _():
+            exchange((SPARE, halves[k]), 0).start()
+
+    def start(i):
+        exchange(i, i // (chunks - 1)).start()
+
+    order = [i for i in range(1, chunks) if i != SPARE]
+
+    def ready(i):
+        if i < KEEP:
+
+            @pl.when(jnp.logical_or(helper1, ex == 0))
+            def _():
+                start(i)
+
+        elif i <= HOLD:
+
+            @pl.when(jnp.logical_and(jnp.logical_not(helper1), ex == 0))
+            def _():
+                start(i)
+
+        else:
+
+            @pl.when(jnp.logical_not(helper1))
+            def _():
+                start(i)
+
+        if i == HOLD:
+
+            @pl.when(jnp.logical_and(jnp.logical_not(helper1), ex != 0))
+            def _():
+                for j in order:
+                    if j <= HOLD:
+                        start(j)
+
     for m in range(1, micro):
-        send[m] = project(ea[0, m].reshape(experts * slots, -1), epin[...])
-        exchange(m, 0).start()
+        if m != SPARE:
+            send[m] = project(ea[0, m].reshape(experts * slots, -1), epin[...])
+            ready(m)
     loads["pin"].wait()
     for l in range(layers):
         loads["dao", l].wait()
         for m in range(micro):
             i = micro + l * micro + m
             send[i] = project(da[0, l, m], pin[l])
-            exchange(i, i // (chunks - 1)).start()
+            ready(i)
+
+    meetings = {0: 1, 2: 2, 4: 3, 5: 4, 6: 5, 8: 6}
+
+    def meet(step):
+        if step in meetings:
+            listen(meetings[step])
+            if meetings[step] < 6:
+                hello(meetings[step] + 1)
 
     for name in ("epout", "evalid", "dval", "eam", "ec"):
         loads[name].wait()
     for m in range(micro):
-        pl.semaphore_wait(here.at[m], len(rounds[m]))
-        if m + 1 < len(rounds):
-            hello(here.at[m + 1], rounds[m + 1])
+        meet(m)
         u = project(ea[1, m].reshape(experts * slots, -1), epin[...])
         w = project(ec[m].reshape(experts * slots, -1), epout[...])
         parts = [
@@ -184,12 +316,27 @@
         wv_i = jnp.concatenate(parts, axis=0)
         wv[m] = wv_i
         acc[m] = fold(u * wv_i)
+        if m == 1:
+            for k, helper in enumerate((helper1, helper2)):
+
+                @pl.when(helper)
+                def _():
+                    give(k).wait_recv()
+                    pass_on(k).start()
+
+            @pl.when(helper1)
+            def _():
+                for j in order:
+                    if j >= KEEP:
+                        start(j)
+
     loads["pout"].wait()
     for l in range(layers):
         loads["dam", l].wait()
         loads["dc", l].wait()
         for m in range(micro):
             i = micro + l * micro + m
+            meet(i)
             u = project(da[1, l, m], pin[l])
             w = project(dc[l, m], pout[l])
             wv_i = lax.dot_general(
@@ -197,6 +344,14 @@
             )
             wv[i] = wv_i
             acc[m] += fold(u * wv_i)
+            if i == 7:
+                for k, helper in enumerate((helper1, helper2)):
+
+                    @pl.when(helper)
+                    def _():
+                        pass_on(k).wait_recv()
+                        deliver(k).start()
+
     loads["ids"].wait()
     loads["prior"].wait()
     domains = prior_mix.shape[0]
@@ -237,7 +392,7 @@
     ][1:]
     offsets.sort(key=hops, reverse=True)
     targets = [away(offset) for offset in offsets]
-    for k, first in enumerate((0, n_t)):
+    for k, first in enumerate((n_t, 0)):
         first = jnp.where(me == first, targets[k], first)
         targets[k + 1 :] = [jnp.where(t == first, targets[k], t) for t in targets[k + 1 :]]
         targets[k] = first
@@ -271,6 +426,12 @@
 
     everyone.wait_send()
     exchange(pl.ds(0, chunks), 0).wait_send()
+    for k, helper in enumerate((helper1, helper2)):
+
+        @pl.when(helper)
+        def _():
+            pass_on(k).wait_send()
+            deliver(k).wait_send()
 
 
 def per_device(*args):
@@ -322,7 +483,10 @@
             pltpu.VMEM((micro, 8, rank), F32),
             pltpu.VMEM((1, 128), F32),
             pltpu.VMEM((devices, 1, 128), F32),
-            pltpu.SemaphoreType.REGULAR((4,)),
+            pltpu.VMEM((2, half // 2, rank), F32),
+            pltpu.VMEM((2, half // 2, rank), F32),
+            pltpu.SemaphoreType.DMA((4, 2)),
+            pltpu.SemaphoreType.REGULAR((6,)),
             pltpu.SemaphoreType.DMA((n_loads,)),
             pltpu.SemaphoreType.DMA,
             pltpu.SemaphoreType.DMA((2,)),

time: 32.8 us -> 31.6 us (0.963)
  Pallas kernels: 32.1 us -> 31 us
    pallas_call x1, Pallas kernels: 32.1 us -> 31 us  [per_device(): pl.pallas_call(functools.partial(kernel, sizes), out_shape=jax.ShapeDtype...]
where the time goes in v4:
time: 31.6 us; the launch traced here: 31.5 us
  Pallas kernels  31 us (98%)
  local copies, waits for them, and re-layouts  0.51 us (2%)
    pallas_call x1, Pallas kernels, per_device(): pl.pallas_call(functools.partial(kernel, sizes), out_shape=jax.ShapeDtype...  31 us

profile of v4, /device:TPU:1, one launch (start us, length us, event | category | flops | bytes accessed | tf_op | source)
XLA Modules:
  0.0 31.5 jit_solution(13042210080627103776)
XLA Ops:
  0.0 31.0 %align.1 = f32[2]{0:T(128)S(1)} custom-call(bf16[2,4,256,1792]{3,2,1,0:T(8,128)(2,1)} %dense_act.1, bf16[2,4,128,3584]{3,2,1,0:T(8,128)(2,1)} %dense_cot.1, bf16[2,1792,128]{2,1,0:T(8,128)(2,1)} %dense_proj_in.1, bf16[2,3584,128]{2,1,0:T(8,128)(2,1)} %dense_proj_out.1, bf16[4,4,64,1280]{3,2,1,0:T(8,128)(2,1)} %expert_act.1, ...), custom_call_target="tpu_custom_call" | custom-call | tf_op jit(solution)/shard_map/align/pallas_call | solution.py:462
  31.0 0.5 %copy.14 = f32[2]{0:T(128)} copy(f32[2]{0:T(128)S(1)} %align.1) | data formatting | bytes 16

commit v5 on v4

--- a/solution.py
+++ b/solution.py
@@ -9,9 +9,12 @@
 
 MESH = pl.DeviceIdType.MESH
 F32 = jnp.float32
-HOLD = 8
+HOLD = 10
 KEEP = 6
-SPARE = 3
+SPARE = (3, 2)
+PASS = 3
+DELIVER = (6, 7,)
+LIMITS = (21, 26)
 EXACT = lax.Precision.HIGHEST
 
 
@@ -95,13 +98,18 @@
         def _():
             signal(semaphore, target)
 
-    age = y + 2 * z
     mate, sibling, across = number(ex, x + 1 - 2 * te, y, z), number(1 - ex, x, y, z), number(ex, last - x, y, z)
-    mirror = number(ex, x, last - y, last - z)
+    mirror = number(ex, last - x, last - y, last - z)
     up_y, down_y = number(ex, x, (y + 1) % ring, z), number(ex, x, (y + last) % ring, z)
     up_z, down_z = number(ex, x, y, (z + 1) % ring), number(ex, x, y, (z + last) % ring)
-    giver2, giver1 = age >= 8, age >= 6
-    helper2, helper1 = age <= 1, age <= 3
+
+    def late(xx, yy, zz):
+        return 5 * (xx // n_t) + 5 * yy - 4 * (yy // last) + 6 * zz - 4 * (zz // last)
+
+    mine_late, mirror_late = late(x, y, z), late(last - x, last - y, last - z)
+    givers = [mine_late >= limit for limit in LIMITS]
+    helpers = [mirror_late >= limit for limit in LIMITS]
+    helping = helpers[0]
 
     def hello(k):
         if k == 0:
@@ -109,7 +117,7 @@
             signal(semaphore, mate)
             signal(semaphore, sibling)
             signal_if(x < n_t, semaphore, across)
-            signal_if(helper1, semaphore, mirror)
+            signal_if(helping, semaphore, mirror)
         else:
             semaphore = here.at[k - 1]
         if k == 1:
@@ -132,7 +140,7 @@
     from_below = (y + last) // ring + (z + last) // ring
     from_above = 2 - y // last - z // last
     heard = {
-        0: 2 + from_below + x // n_t + age // 6,
+        0: 2 + from_below + x // n_t + jnp.where(givers[0], 1, 0),
         1: from_above + 1 - x // n_t,
         2: 3 + from_below + from_above,
         3: 3 + from_below + from_above,
@@ -200,6 +208,7 @@
         return jnp.dot(block, weight, preferred_element_type=F32)
 
     halves = (pl.ds(0, half // 2), pl.ds(half // 2, half // 2))
+    units = [(i, part) for i in SPARE for part in halves][: len(LIMITS)]
 
     def hop(source, target, sent, arrived, device):
         return pltpu.make_async_remote_copy(
@@ -212,14 +221,14 @@
         )
 
     def give(k):
-        return hop(send.at[SPARE, halves[k]], relay_a.at[k], send_sem, relay_sem.at[0, k], mirror)
+        return hop(send.at[units[k]], relay_a.at[k], send_sem, relay_sem.at[0, k], mirror)
 
     def pass_on(k):
         return hop(relay_a.at[k], relay_b.at[k], relay_sem.at[1, k], relay_sem.at[2, k], mate)
 
     def deliver(k):
         return hop(
-            relay_b.at[k], recv.at[SPARE, halves[k]], relay_sem.at[3, k], recv_sem.at[0], mirror
+            relay_b.at[k], recv.at[units[k]], relay_sem.at[3, k], recv_sem.at[0], mirror
         )
 
     loads["epin"].wait()
@@ -234,51 +243,79 @@
     send[0, tail] = project(ea[0, 0, 1:].reshape((experts - 1) * slots, -1), epin[...])
     exchange((0, tail), 0).start()
     loads["eao"].wait()
-    send[SPARE] = project(ea[0, SPARE].reshape(experts * slots, -1), epin[...])
-    for k, giver in enumerate((giver1, giver2)):
-
-        @pl.when(giver)
-        def _():
-            give(k).start()
-
-        @pl.when(jnp.logical_not(giver))
-        def _():
-            exchange((SPARE, halves[k]), 0).start()
+    for i in SPARE:
+        send[i] = project(ea[0, i].reshape(experts * slots, -1), epin[...])
+        for part in halves:
+            if (i, part) not in units:
+
+                @pl.when(ex == 0)
+                def _():
+                    exchange((i, part), 0).start()
+
+                continue
+            k = units.index((i, part))
+
+            @pl.when(givers[k])
+            def _():
+                give(k).start()
+
+            direct = jnp.logical_not(givers[k])
+
+            @pl.when(jnp.logical_and(direct, ex == 0) if i != SPARE[0] else direct)
+            def _():
+                exchange(units[k], 0).start()
 
     def start(i):
         exchange(i, i // (chunks - 1)).start()
 
-    order = [i for i in range(1, chunks) if i != SPARE]
+    order = [i for i in range(1, chunks) if i not in SPARE]
 
     def ready(i):
         if i < KEEP:
 
-            @pl.when(jnp.logical_or(helper1, ex == 0))
+            @pl.when(ex == 0)
             def _():
                 start(i)
 
         elif i <= HOLD:
 
-            @pl.when(jnp.logical_and(jnp.logical_not(helper1), ex == 0))
+            @pl.when(jnp.logical_and(jnp.logical_not(helping), ex == 0))
             def _():
                 start(i)
 
         else:
 
-            @pl.when(jnp.logical_not(helper1))
+            @pl.when(jnp.logical_not(helping))
             def _():
                 start(i)
 
         if i == HOLD:
 
-            @pl.when(jnp.logical_and(jnp.logical_not(helper1), ex != 0))
+            @pl.when(ex != 0)
             def _():
                 for j in order:
-                    if j <= HOLD:
+                    if j < KEEP:
                         start(j)
 
+            for j in SPARE[1:]:
+                for part in halves:
+                    held = ex != 0
+                    if (j, part) in units:
+                        giving = givers[units.index((j, part))]
+                        held = jnp.logical_and(held, jnp.logical_not(giving))
+
+                    @pl.when(held)
+                    def _():
+                        exchange((j, part), 0).start()
+
+            @pl.when(jnp.logical_and(jnp.logical_not(helping), ex != 0))
+            def _():
+                for j in order:
+                    if KEEP <= j <= HOLD:
+                        start(j)
+
     for m in range(1, micro):
-        if m != SPARE:
+        if m not in SPARE:
             send[m] = project(ea[0, m].reshape(experts * slots, -1), epin[...])
             ready(m)
     loads["pin"].wait()
@@ -296,6 +333,29 @@
             listen(meetings[step])
             if meetings[step] < 6:
                 hello(meetings[step] + 1)
+
+    def relay(step):
+        if step == PASS:
+            for k, helper in enumerate(helpers):
+
+                @pl.when(helper)
+                def _():
+                    give(k).wait_recv()
+                    pass_on(k).start()
+
+            @pl.when(helping)
+            def _():
+                for j in order:
+                    if j >= KEEP:
+                        start(j)
+
+        for k, helper in enumerate(helpers):
+            if step == DELIVER[k]:
+
+                @pl.when(helper)
+                def _():
+                    pass_on(k).wait_recv()
+                    deliver(k).start()
 
     for name in ("epout", "evalid", "dval", "eam", "ec"):
         loads[name].wait()
@@ -316,20 +376,7 @@
         wv_i = jnp.concatenate(parts, axis=0)
         wv[m] = wv_i
         acc[m] = fold(u * wv_i)
-        if m == 1:
-            for k, helper in enumerate((helper1, helper2)):
-
-                @pl.when(helper)
-                def _():
-                    give(k).wait_recv()
-                    pass_on(k).start()
-
-            @pl.when(helper1)
-            def _():
-                for j in order:
-                    if j >= KEEP:
-                        start(j)
-
+        relay(m)
     loads["pout"].wait()
     for l in range(layers):
         loads["dam", l].wait()
@@ -344,14 +391,7 @@
             )
             wv[i] = wv_i
             acc[m] += fold(u * wv_i)
-            if i == 7:
-                for k, helper in enumerate((helper1, helper2)):
-
-                    @pl.when(helper)
-                    def _():
-                        pass_on(k).wait_recv()
-                        deliver(k).start()
-
+            relay(i)
     loads["ids"].wait()
     loads["prior"].wait()
     domains = prior_mix.shape[0]
@@ -426,7 +466,7 @@
 
     everyone.wait_send()
     exchange(pl.ds(0, chunks), 0).wait_send()
-    for k, helper in enumerate((helper1, helper2)):
+    for k, helper in enumerate(helpers):
 
         @pl.when(helper)
         def _():
@@ -483,9 +523,9 @@
             pltpu.VMEM((micro, 8, rank), F32),
             pltpu.VMEM((1, 128), F32),
             pltpu.VMEM((devices, 1, 128), F32),
-            pltpu.VMEM((2, half // 2, rank), F32),
-            pltpu.VMEM((2, half // 2, rank), F32),
-            pltpu.SemaphoreType.DMA((4, 2)),
+            pltpu.VMEM((len(LIMITS), half // 2, rank), F32),
+            pltpu.VMEM((len(LIMITS), half // 2, rank), F32),
+            pltpu.SemaphoreType.DMA((4, len(LIMITS))),
             pltpu.SemaphoreType.REGULAR((6,)),
             pltpu.SemaphoreType.DMA((n_loads,)),
             pltpu.SemaphoreType.DMA,

time: 31.6 us -> 31.1 us (0.984)
  Pallas kernels: 31 us -> 30.4 us
    pallas_call x1, Pallas kernels: 31 us -> 30.4 us  [per_device(): pl.pallas_call(functools.partial(kernel, sizes), out_shape=jax.ShapeDtype...]
where the time goes in v5:
time: 31.1 us; the launch traced here: 31 us
  Pallas kernels  30.4 us (98%)
  local copies, waits for them, and re-layouts  0.51 us (2%)
    pallas_call x1, Pallas kernels, per_device(): pl.pallas_call(functools.partial(kernel, sizes), out_shape=jax.ShapeDtype...  30.4 us

profile of v5, /device:TPU:1, one launch (start us, length us, event | category | flops | bytes accessed | tf_op | source)
XLA Modules:
  0.0 31.0 jit_solution(5844360854713964232)
XLA Ops:
  0.0 30.4 %align.1 = f32[2]{0:T(128)S(1)} custom-call(bf16[2,4,256,1792]{3,2,1,0:T(8,128)(2,1)} %dense_act.1, bf16[2,4,128,3584]{3,2,1,0:T(8,128)(2,1)} %dense_cot.1, bf16[2,1792,128]{2,1,0:T(8,128)(2,1)} %dense_proj_in.1, bf16[2,3584,128]{2,1,0:T(8,128)(2,1)} %dense_proj_out.1, bf16[4,4,64,1280]{3,2,1,0:T(8,128)(2,1)} %expert_act.1, ...), custom_call_target="tpu_custom_call" | custom-call | tf_op jit(solution)/shard_map/align/pallas_call | solution.py:502
  30.4 0.5 %copy.14 = f32[2]{0:T(128)} copy(f32[2]{0:T(128)S(1)} %align.1) | data formatting | bytes 16

commit v6 on v5

--- a/solution.py
+++ b/solution.py
@@ -9,12 +9,12 @@
 
 MESH = pl.DeviceIdType.MESH
 F32 = jnp.float32
-HOLD = 10
-KEEP = 6
+HOLD = 8
+KEEP = 5
 SPARE = (3, 2)
-PASS = 3
-DELIVER = (6, 7,)
-LIMITS = (21, 26)
+PASS = 2
+DELIVER = (5, 6, 7,)
+LIMITS = (21, 24, 28)
 EXACT = lax.Precision.HIGHEST
 
 
@@ -167,7 +167,11 @@
     rest = pl.ds(1, micro - 1)
     plan = {
         "epin": (expert_proj_in, epin),
-        "eao0": (expert_act.at[0, :, pl.ds(e_other, slots), :], ea.at[0, 0]),
+        "first": (expert_act.at[0, 0, pl.ds(e_other, slots), :], ea.at[0, 0, 0]),
+        "eao0": (
+            expert_act.at[0, pl.ds(1, experts - 1), pl.ds(e_other, slots), :],
+            ea.at[0, 0, pl.ds(1, experts - 1)],
+        ),
         "eao": (expert_act.at[rest, :, pl.ds(e_other, slots), :], ea.at[0, rest]),
         "pin": (dense_proj_in, pin),
         ("dao", 0): (dense_act.at[0, :, pl.ds(other, half), :], da.at[0, 0]),
@@ -189,7 +193,7 @@
     loads = {
         name: pltpu.make_async_copy(*plan[name], load_sem.at[k]) for k, name in enumerate(names)
     }
-    for name in names[:6]:
+    for name in names[:7]:
         loads[name].start()
 
     hello(0)
@@ -232,14 +236,15 @@
         )
 
     loads["epin"].wait()
-    loads["eao0"].wait()
+    loads["first"].wait()
     head, tail = pl.ds(0, slots), pl.ds(slots, (experts - 1) * slots)
     send[0, head] = project(ea[0, 0, 0], epin[...])
     listen(0)
     exchange((0, head), 0).start()
-    for name in names[6:]:
+    for name in names[7:]:
         loads[name].start()
     hello(1)
+    loads["eao0"].wait()
     send[0, tail] = project(ea[0, 0, 1:].reshape((experts - 1) * slots, -1), epin[...])
     exchange((0, tail), 0).start()
     loads["eao"].wait()
@@ -412,12 +417,17 @@
         for i in range(m, chunks - 1, micro):
             s += fold(recv[i] * wv[i])
         sums.append(s)
+    def row_of(m, partial):
+        s = jnp.sum(jnp.sum(partial, axis=0, keepdims=True), axis=1, keepdims=True)
+        return jnp.where(lane == ids[m], s, 0.0)
+
+    mine_row = row_of(0, sums[0])
+    for m in range(1, micro - 1):
+        mine_row += row_of(m, sums[m])
+    row[...] = mine_row
     exchange(chunks - 1, 1).wait_recv()
     sums[micro - 1] += fold(recv[chunks - 1] * wv[chunks - 1])
-    mine_row = jnp.zeros((1, 128), F32)
-    for m in range(micro):
-        s = jnp.sum(jnp.sum(sums[m], axis=0, keepdims=True), axis=1, keepdims=True)
-        mine_row += jnp.where(lane == ids[m], s, 0.0)
+    mine_row = row[...] + row_of(micro - 1, sums[micro - 1])
 
     row[...] = mine_row
     rows[me] = mine_row
@@ -498,7 +508,7 @@
     rank = dense_proj_in.shape[2]
     bf = dense_act.dtype
     chunks = micro + layers * micro
-    n_loads = 18
+    n_loads = 19
     return pl.pallas_call(
         functools.partial(kernel, sizes),
         out_shape=jax.ShapeDtypeStruct((prior_mix.shape[0] // sizes[0],), F32),

time: 31.1 us -> 30.9 us (level)
  no operation moved by 1% of the time
where the time goes in v6:
time: 30.9 us; the launch traced here: 30.8 us
  Pallas kernels  30.3 us (98%)
  local copies, waits for them, and re-layouts  0.51 us (2%)
    pallas_call x1, Pallas kernels, per_device(): pl.pallas_call(functools.partial(kernel, sizes), out_shape=jax.ShapeDtype...  30.3 us

profile of v6, /device:TPU:1, one launch (start us, length us, event | category | flops | bytes accessed | tf_op | source)
XLA Modules:
  0.0 30.8 jit_solution(1026204712510030648)
XLA Ops:
  0.0 30.3 %align.1 = f32[2]{0:T(128)S(1)} custom-call(bf16[2,4,256,1792]{3,2,1,0:T(8,128)(2,1)} %dense_act.1, bf16[2,4,128,3584]{3,2,1,0:T(8,128)(2,1)} %dense_cot.1, bf16[2,1792,128]{2,1,0:T(8,128)(2,1)} %dense_proj_in.1, bf16[2,3584,128]{2,1,0:T(8,128)(2,1)} %dense_proj_out.1, bf16[4,4,64,1280]{3,2,1,0:T(8,128)(2,1)} %expert_act.1, ...), custom_call_target="tpu_custom_call" | custom-call | tf_op jit(solution)/shard_map/align/pallas_call | solution.py:512
  30.3 0.5 %copy.14 = f32[2]{0:T(128)} copy(f32[2]{0:T(128)S(1)} %align.1) | data formatting | bytes 16
